TPU v7x, 32 devices: a whole 2x2x4 slice. The times are simulated.
32 devices in a mesh: groups: 2 (over y), seq: 4 (over z), batch: 4 (over x, core).
Axes of the slice: x: 2, y: 2, z: 4, core: 2. Of those that a mesh axis runs over, the one named last changes fastest.
Arguments:
- queries: bfloat16 [8, 512, 2048], P(('groups', 'batch'), 'seq'), parts along dimension 0, may hold values from -80 to 80, as said below
- keys: bfloat16 [8, 512, 512], P(('groups', 'batch'), 'seq'), parts along dimension 0, may hold values from -4.5 to 4.5
- values: bfloat16 [8, 512, 512], P(('groups', 'batch'), 'seq'), parts along dimension 0, may hold values from -6 to 6
Outputs:
- attended: bfloat16 [8, 512, 2048], P(('groups', 'batch'), 'seq'), parts along dimension 0
There are 2 independent parts, one for each index of `groups`. A program takes and returns all parts, laid end to end along the dimension named above; each array names one. Nothing has to cross between parts.
Inputs may be any that keep to these rules, and one draw needn't show every extreme that they name: `queries`: query vectors of order a few units; a few positions may hold much larger entries.
All inputs are finite; a program needn't handle non-finite values.
Results may differ from a plain program's by a relative error of at most 0.009.
Values may be sent and summed in bfloat16 or wider, within the bound.
A program may use at most 64 MiB of HBM per device.

v0:
```python
import functools
import math

import jax
import jax.numpy as jnp
from jax import lax
from jax.experimental import pallas as pl
from jax.experimental.pallas import tpu as pltpu
from jax.sharding import PartitionSpec as P

HEAD_SIZE = 128
SCALE = math.log2(math.e) / math.sqrt(HEAD_SIZE)
MESH = pl.DeviceIdType.MESH


def kernel(
    n, groups, per_group,
    q_hbm, k_hbm, v_hbm, o,
    q, kv, m, acc,
    load_sem, q_sem, send_sem, recv_sem,
):
    rows = q.shape[0]
    me = lax.axis_index("seq")
    right, left = lax.rem(me + 1, n), lax.rem(me + n - 1, n)

    def loads(g):
        cols = pl.ds(g * HEAD_SIZE, HEAD_SIZE)
        return (
            pltpu.make_async_copy(
                k_hbm.at[0, :, cols], kv.at[0, g, pl.ds(0, rows)], load_sem.at[0, g]
            ),
            pltpu.make_async_copy(
                v_hbm.at[0, :, cols], kv.at[0, g, pl.ds(rows, rows)], load_sem.at[1, g]
            ),
        )

    def send(slot, g):
        return pltpu.make_async_remote_copy(
            src_ref=kv.at[slot, g],
            dst_ref=kv.at[slot + 1, g],
            send_sem=send_sem.at[slot, g],
            recv_sem=recv_sem.at[slot + 1, g],
            device_id={"seq": right},
            device_id_type=MESH,
        )

    def receive(slot, g):
        return pltpu.make_async_remote_copy(
            src_ref=kv.at[slot, g],
            dst_ref=kv.at[slot, g],
            send_sem=send_sem.at[slot, g],
            recv_sem=recv_sem.at[slot, g],
            device_id={"seq": right},
            device_id_type=MESH,
        )

    q_copy = pltpu.make_async_copy(q_hbm.at[0], q, q_sem)

    barrier = pltpu.get_barrier_semaphore()

    @pl.when(me > 0)
    def _():
        pl.semaphore_signal(barrier, inc=1, device_id={"seq": left}, device_id_type=MESH)

    for g in range(groups):
        for copy in loads(g):
            copy.start()
    q_copy.start()

    @pl.when(me < n - 1)
    def _():
        pl.semaphore_wait(barrier, 1)

    for g in range(groups):
        for copy in loads(g):
            copy.wait()

        @pl.when(me < n - 1)
        def _():
            send(0, g).start()

    q_copy.wait()

    def scores_of(slot, g):
        stacked = jnp.concatenate(
            [
                q[:, (g * per_group + h) * HEAD_SIZE : (g * per_group + h + 1) * HEAD_SIZE]
                for h in range(per_group)
            ],
            axis=0,
        )
        return lax.dot_general(
            stacked,
            kv[slot, g, :rows, :],
            (((1,), (1,)), ((), ())),
            preferred_element_type=jnp.float32,
        )

    def weighted(p, slot, g):
        block = jnp.concatenate(
            [kv[slot, g, rows:, :], jnp.ones((rows, HEAD_SIZE), jnp.bfloat16)], axis=1
        )
        return jnp.dot(p.astype(jnp.bfloat16), block, preferred_element_type=jnp.float32)

    def finish(total, g):
        done = (total[:, :HEAD_SIZE] / total[:, HEAD_SIZE:]).astype(jnp.bfloat16)
        for h in range(per_group):
            at = (g * per_group + h) * HEAD_SIZE
            o[0, :, at : at + HEAD_SIZE] = done[h * rows : (h + 1) * rows]

    row = lax.rem(lax.broadcasted_iota(jnp.int32, (per_group * rows, rows), 0), rows)
    visible = lax.broadcasted_iota(jnp.int32, (per_group * rows, rows), 1) <= row

    for g in range(groups):
        s = jnp.where(visible, scores_of(0, g), -1e30)
        new_m = jnp.max(s, axis=1, keepdims=True)
        total = weighted(jnp.exp2((s - new_m) * SCALE), 0, g)
        acc[g] = total
        m[g] = jnp.broadcast_to(new_m, m.shape[1:])

        @pl.when(me == 0)
        def _():
            finish(acc[g], g)

    @pl.loop(1, me + 1)
    def _(slot):
        for g in range(groups):
            receive(slot, g).wait_recv()

            @pl.when(me < n - 1)
            def _():
                send(slot, g).start()

            s = scores_of(slot, g)
            old_m = m[g]
            new_m = jnp.maximum(old_m, jnp.max(s, axis=1, keepdims=True))
            fade = jnp.exp2((old_m - new_m) * SCALE)
            p = jnp.exp2((s - new_m[:, :1]) * SCALE)
            total = acc[g] * jnp.concatenate([fade, fade], axis=1) + weighted(p, slot, g)

            @pl.when(slot < me)
            def _():
                acc[g] = total
                m[g] = new_m

            @pl.when(slot == me)
            def _():
                finish(total, g)

    @pl.when(me < n - 1)
    def _():
        @pl.loop(0, me + 1)
        def _(slot):
            for g in range(groups):
                send(slot, g).wait_send()


def on_device(n, queries, keys, values):
    rows, query_width = queries.shape[1:]
    groups = keys.shape[2] // HEAD_SIZE
    per_group = query_width // HEAD_SIZE // groups
    hbm = pl.BlockSpec(memory_space=pltpu.HBM)
    held = (2 * rows * query_width + 2 * n * rows * keys.shape[2]) * 2 + 3 * rows * query_width * 4
    return pl.pallas_call(
        functools.partial(kernel, n, groups, per_group),
        out_shape=jax.ShapeDtypeStruct(queries.shape, queries.dtype),
        in_specs=[hbm, hbm, hbm],
        out_specs=pl.BlockSpec(memory_space=pltpu.VMEM),
        scratch_shapes=[
            pltpu.VMEM((rows, query_width), jnp.bfloat16),
            pltpu.VMEM((n, groups, 2 * rows, HEAD_SIZE), jnp.bfloat16),
            pltpu.VMEM((groups, per_group * rows, HEAD_SIZE), jnp.float32),
            pltpu.VMEM((groups, per_group * rows, 2 * HEAD_SIZE), jnp.float32),
            pltpu.SemaphoreType.DMA((2, groups)),
            pltpu.SemaphoreType.DMA,
            pltpu.SemaphoreType.DMA((n, groups)),
            pltpu.SemaphoreType.DMA((n, groups)),
        ],
        compiler_params=pltpu.CompilerParams(collective_id=0, has_side_effects=True, vmem_limit_bytes=held + 4 * 2**20),
    )(*(pltpu.with_memory_space_constraint(x, pltpu.HBM) for x in (queries, keys, values)))


def solution(mesh):
    spec = P(("groups", "batch"), "seq", None)
    return jax.shard_map(
        functools.partial(on_device, mesh.shape["seq"]),
        mesh=mesh,
        in_specs=(spec, spec, spec),
        out_specs=spec,
        check_vma=False,
    )
```

profile of v0, /device:TPU:24, one launch (start us, length us, event | category | flops | bytes accessed | tf_op | source)
XLA Modules:
  0.0 21.1 jit_solution(12497606741375655877)
XLA Ops:
  0.0 20.3 %shard_map.37 = bf16[1,128,2048]{2,1,0:T(8,128)(2,1)S(1)} custom-call(bf16[1,128,2048]{2,1,0:T(8,128)(2,1)} %q_hbm.1, bf16[1,128,512]{2,1,0:T(8,128)(2,1)} %k_hbm.1, bf16[1,128,512]{2,1,0:T(8,128)(2,1)} %v_hbm.1), custom_call_target="tpu_custom_call" | custom-call | tf_op jit(solution)/shard_map/pallas_call | solution.py:164
  20.3 0.8 %copy.5 = bf16[1,128,2048]{2,1,0:T(8,128)(2,1)} copy(bf16[1,128,2048]{2,1,0:T(8,128)(2,1)S(1)} %shard_map.37) | data formatting | bytes 1048576
where the time goes:
time: 21.2 us; the launch traced here: 21.1 us
  Pallas kernels  20.3 us (96%)
  local copies, waits for them, and re-layouts  0.8 us (4%)
    pallas_call x1, Pallas kernels, on_device(): pl.pallas_call(functools.partial(kernel, n, groups, per_group), out_shape...  20.3 us
    unnamed x1, local copies, waits for them, and re-layouts  0.8 us

commit v1 on v0

--- a/solution.py
+++ b/solution.py
@@ -11,6 +11,442 @@
 HEAD_SIZE = 128
 SCALE = math.log2(math.e) / math.sqrt(HEAD_SIZE)
 MESH = pl.DeviceIdType.MESH
+
+SCHEDULED = 4
+
+FIRST, NEXT, MERGE = range(3)
+KEEP, FINISH, RETURN = range(3)
+CODE = 2**14
+
+
+def pack(op, slot, g, answer=0, wait=0, forward=0, then=0, flag=KEEP):
+    code = 0
+    for value, size in ((flag, 4), (then, 8), (forward, 2), (wait, 2), (answer, 2), (g, 4), (slot, 4), (op, 4)):
+        code = code * size + value
+    return code
+
+
+def moved_heads(n, groups, phase):
+    return 0 if n < 4 else groups // (2 if phase == 0 else 4)
+
+
+def order_of(top, groups, moved, phase):
+    stay = list(range(moved, groups))
+    older = range(top - 1, -1, -1)
+    if phase == 0 and moved:
+        out = [(top, 0)] + [(top, g) for g in stay] + [(b, 0) for b in older]
+        for g in range(1, moved):
+            out += [(b, g) for b in range(top, -1, -1)]
+        return out + [(b, g) for b in older for g in stay]
+    ahead = [(top, g) for g in stay[1:]]
+    out = [(top, stay[0])]
+    behind = [(b, g) for b in older for g in stay[1:] + stay[:1]]
+    for i, unit in enumerate(behind):
+        out += [unit] + (ahead[i - 1 : i] if 0 < i else [])
+    out += ahead[max(len(behind) - 1, 0) :]
+    for g in range(moved):
+        out += [(b, g) for b in [*older, top]]
+    return out
+
+
+def script(n, groups, phase, rank):
+    moved = moved_heads(n, groups, phase)
+    helper, last = n - 2, n - 1
+    order = order_of(max(n - 3, 0), groups, moved, phase)
+
+    def sends(r):
+        mine = [(b, g) for b, g in order if b <= r]
+        if r < helper:
+            return mine
+        own = [(r, g) for g in range(moved, groups)]
+        return own + [(b, g) for b, g in mine if g >= moved]
+
+    queue = sends(rank) if rank < last else []
+    arrivals = sends(helper) if rank == last else [(b, g) for b, g in order if b < rank]
+    before = []
+    while queue and queue[0][0] == rank:
+        before.append(queue.pop(0)[1])
+
+    steps = []
+    left = {g: rank for g in range(groups)}
+    waiting = {g: rank for g in range(moved)} if rank == helper else {}
+    seen = {g: [] for g in waiting}
+    ready = set()
+    returned = 0
+
+    def start_answer(g):
+        ready.add(g)
+        steps.append(pack(FIRST, 0, g, answer=1))
+        for slot in seen[g]:
+            steps.append(pack(NEXT, slot, g, answer=1))
+
+    for i, (b, g) in enumerate(arrivals):
+        slot = rank - b
+        how = dict(wait=1)
+        if queue and queue[0] == (b, g):
+            queue.pop(0)
+            how["forward"] = 1
+            if queue and queue[0][0] == rank:
+                how["then"] = queue.pop(0)[1] + 1
+        left[g] -= 1
+        if g in waiting:
+            waiting[g] -= 1
+            if g in ready:
+                steps.append(pack(NEXT, slot, g, answer=1, flag=KEEP if waiting[g] else RETURN, **how))
+                how = {}
+            seen[g].append(slot)
+        ends = left[g] == 0 and not (rank == last and g < moved)
+        steps.append(pack(NEXT, slot, g, flag=FINISH if ends else KEEP, **how))
+        if i + 1 < len(arrivals):
+            h = arrivals[i + 1][1]
+            if h in waiting and waiting[h] == 1:
+                start_answer(h)
+        if rank == last:
+            while returned < moved and returns_before(order, moved, returned, groups) <= i + 1:
+                steps.append(pack(MERGE, 0, returned))
+                returned += 1
+    if rank == last:
+        steps += [pack(MERGE, 0, g) for g in range(returned, moved)]
+    assert not queue
+    return before, steps
+
+
+def returns_before(order, moved, g, groups):
+    at = max(i for i, (_, h) in enumerate(order) if h == g)
+    return groups - moved + sum(1 for _, h in order[:at] if h >= moved)
+
+
+def scheduled_kernel(
+    n, groups, per_group, most,
+    q_hbm, k_hbm, v_hbm, o,
+    q, kv, m, acc, back, back_stats, mine, mine_stats,
+    load_sem, q_sem, send_sem, recv_sem, ask_send, ask_recv, back_send, back_recv,
+):
+    rows = kv.shape[2] // 2
+    tall = per_group * rows
+    me = lax.axis_index("seq")
+    phase = lax.rem(lax.axis_index("batch"), 2)
+    last, helper = n - 1, n - 2
+
+    def kv_load(g):
+        cols = pl.ds(g * HEAD_SIZE, HEAD_SIZE)
+        return (
+            pltpu.make_async_copy(
+                k_hbm.at[0, :, cols], kv.at[0, g, pl.ds(0, rows)], load_sem.at[0, g]
+            ),
+            pltpu.make_async_copy(
+                v_hbm.at[0, :, cols], kv.at[0, g, pl.ds(rows, rows)], load_sem.at[1, g]
+            ),
+        )
+
+    def q_load(g, h):
+        return pltpu.make_async_copy(
+            q_hbm.at[0, :, pl.ds((g * per_group + h) * HEAD_SIZE, HEAD_SIZE)],
+            q.at[g, pl.ds(h * rows, rows)],
+            q_sem.at[g, h],
+        )
+
+    def send(slot, g):
+        return pltpu.make_async_remote_copy(
+            src_ref=kv.at[slot, g],
+            dst_ref=kv.at[slot + 1, g],
+            send_sem=send_sem.at[slot, g],
+            recv_sem=recv_sem.at[slot + 1, g],
+            device_id={"seq": jnp.minimum(me + 1, last)},
+            device_id_type=MESH,
+        )
+
+    def receive(slot, g):
+        return pltpu.make_async_remote_copy(
+            src_ref=kv.at[slot, g],
+            dst_ref=kv.at[slot, g],
+            send_sem=send_sem.at[slot, g],
+            recv_sem=recv_sem.at[slot, g],
+            device_id={"seq": jnp.minimum(me + 1, last)},
+            device_id_type=MESH,
+        )
+
+    def ask(g):
+        return pltpu.make_async_remote_copy(
+            src_ref=q.at[g],
+            dst_ref=q.at[groups + g],
+            send_sem=ask_send.at[g],
+            recv_sem=ask_recv.at[g],
+            device_id={"seq": jnp.int32(helper)},
+            device_id_type=MESH,
+        )
+
+    def give(g):
+        return (
+            pltpu.make_async_remote_copy(
+                src_ref=mine.at[g],
+                dst_ref=back.at[g],
+                send_sem=back_send.at[0, g],
+                recv_sem=back_recv.at[0, g],
+                device_id={"seq": jnp.int32(last)},
+                device_id_type=MESH,
+            ),
+            pltpu.make_async_remote_copy(
+                src_ref=mine_stats.at[g],
+                dst_ref=back_stats.at[g],
+                send_sem=back_send.at[1, g],
+                recv_sem=back_recv.at[1, g],
+                device_id={"seq": jnp.int32(last)},
+                device_id_type=MESH,
+            ),
+        )
+
+    barrier = pltpu.get_barrier_semaphore()
+
+    @pl.when(me > 0)
+    def _():
+        pl.semaphore_signal(barrier, inc=1, device_id={"seq": me - 1}, device_id_type=MESH)
+
+    if most:
+        @pl.when(me == helper)
+        def _():
+            pl.semaphore_signal(barrier, inc=1, device_id={"seq": jnp.int32(last)}, device_id_type=MESH)
+
+    for g in range(groups):
+        for copy in kv_load(g):
+            copy.start()
+    for g in range(groups):
+        for h in range(per_group):
+            q_load(g, h).start()
+
+    scripts = {(r, p): script(n, groups, p, r) for r in range(n) for p in range(2)}
+    here = {key: (me == key[0]) & (phase == key[1]) for key in scripts}
+
+    def pick(values):
+        out = jnp.int32(0)
+        for key, value in values.items():
+            if value:
+                out = jnp.where(here[key], jnp.int32(value), out)
+        return out
+
+    count = pick({key: len(steps) for key, (_, steps) in scripts.items()})
+    longest = max(len(steps) for _, steps in scripts.values())
+    words = []
+    for at in range(0, longest, 2):
+        pairs = {key: (steps[at : at + 2] + [0, 0])[:2] for key, (_, steps) in scripts.items()}
+        words.append(pick({key: low + CODE * high for key, (low, high) in pairs.items()}))
+
+    @pl.when(me < last if not most else me >= 0)
+    def _():
+        pl.semaphore_wait(barrier, 1)
+
+    for key, (before, _) in scripts.items():
+        rank, p = key
+
+        @pl.when(here[key])
+        def _(rank=rank, p=p, before=before):
+            if rank == last:
+                for g in range(moved_heads(n, groups, p)):
+                    for h in range(per_group):
+                        q_load(g, h).wait()
+                    ask(g).start()
+            for g in before:
+                for copy in kv_load(g):
+                    copy.wait()
+                send(0, g).start()
+            for g in range(groups):
+                if g not in before:
+                    for copy in kv_load(g):
+                        copy.wait()
+            for g in range(groups):
+                if rank < last or g >= moved_heads(n, groups, p):
+                    for h in range(per_group):
+                        q_load(g, h).wait()
+
+    def scores_of(slot, g, qi):
+        return lax.dot_general(
+            q[qi],
+            kv[slot, g, :rows, :],
+            (((1,), (1,)), ((), ())),
+            preferred_element_type=jnp.float32,
+        )
+
+    def weighted(p, slot, g):
+        block = jnp.concatenate(
+            [kv[slot, g, rows:, :], jnp.ones((rows, HEAD_SIZE), jnp.bfloat16)], axis=1
+        )
+        return jnp.dot(p.astype(jnp.bfloat16), block, preferred_element_type=jnp.float32)
+
+    def write(total, g):
+        done = (total[:, :HEAD_SIZE] / total[:, HEAD_SIZE:]).astype(jnp.bfloat16)
+        for h in range(per_group):
+            at = pl.multiple_of((g * per_group + h) * HEAD_SIZE, HEAD_SIZE)
+            o[0, :, pl.ds(at, HEAD_SIZE)] = done[h * rows : (h + 1) * rows]
+
+    def conclude(qi, g, flag):
+        @pl.when(flag == FINISH)
+        def _():
+            write(acc[qi], g)
+
+        if most:
+            @pl.when(flag == RETURN)
+            def _():
+                total = acc[qi]
+                mine[g] = (total[:, :HEAD_SIZE] / total[:, HEAD_SIZE:]).astype(jnp.bfloat16)
+                lane = lax.broadcasted_iota(jnp.int32, (rows, HEAD_SIZE), 1)
+                stats = jnp.zeros((rows, HEAD_SIZE), jnp.float32)
+                for h in range(per_group):
+                    part = pl.ds(h * rows, rows)
+                    stats = jnp.where(lane == h, m[qi, part, :], stats)
+                    stats = jnp.where(lane == per_group + h, acc[qi, part, HEAD_SIZE:], stats)
+                mine_stats[g] = stats.T[: mine_stats.shape[1]]
+                for copy in give(g):
+                    copy.start()
+
+    row = lax.rem(lax.broadcasted_iota(jnp.int32, (tall, rows), 0), rows)
+    column = lax.broadcasted_iota(jnp.int32, (tall, rows), 1)
+
+    @pl.loop(0, groups + count)
+    def _(i):
+        at = jnp.maximum(i - groups, 0)
+        word = words[0] if words else jnp.int32(0)
+        for j, other in enumerate(words[1:]):
+            word = jnp.where(at >= 2 * (j + 1), other, word)
+        code = jnp.where(lax.rem(at, 2) == 0, lax.rem(word, CODE), lax.div(word, CODE))
+        own = pack(FIRST, 0, 0) + jnp.where(me == 0, pack(FIRST, 0, 0, flag=FINISH), 0) + pack(FIRST, 0, 1) * i
+        code = jnp.where(i < groups, own, code)
+        op = lax.rem(code, 4)
+        slot = lax.rem(lax.div(code, 4), 4)
+        g = lax.rem(lax.div(code, 16), 4)
+        answer = lax.rem(lax.div(code, 64), 2)
+        wait = lax.rem(lax.div(code, 128), 2)
+        forward = lax.rem(lax.div(code, 256), 2)
+        then = lax.rem(lax.div(code, 512), 8)
+        flag = lax.div(code, 4096)
+        qi = g + groups * answer
+
+        @pl.when(wait == 1)
+        def _():
+            receive(slot, g).wait_recv()
+
+            @pl.when(forward == 1)
+            def _():
+                send(slot, g).start()
+
+            @pl.when(then > 0)
+            def _():
+                send(0, then - 1).start()
+
+        if most:
+            @pl.when((op == FIRST) & (answer == 1))
+            def _():
+                ask(g).wait_recv()
+
+        @pl.when(op == FIRST)
+        def _():
+            ahead = rows * answer
+            s = jnp.where(column <= row + ahead, scores_of(0, g, qi), -1e30)
+            new_m = jnp.max(s, axis=1, keepdims=True)
+            acc[qi] = weighted(jnp.exp2((s - new_m) * SCALE), 0, g)
+            m[qi] = jnp.broadcast_to(new_m, m.shape[1:])
+            conclude(qi, g, flag)
+
+        @pl.when(op == NEXT)
+        def _():
+            s = scores_of(slot, g, qi)
+            old_m = m[qi]
+            new_m = jnp.maximum(old_m, jnp.max(s, axis=1, keepdims=True))
+            fade = jnp.exp2((old_m - new_m) * SCALE)
+            p = jnp.exp2((s - new_m[:, :1]) * SCALE)
+            acc[qi] = acc[qi] * jnp.concatenate([fade, fade], axis=1) + weighted(p, slot, g)
+            m[qi] = new_m
+            conclude(qi, g, flag)
+
+        if most:
+            @pl.when(op == MERGE)
+            def _():
+                for copy in give(g):
+                    copy.wait_recv()
+                few = back_stats.shape[1]
+                stats = jnp.concatenate(
+                    [back_stats[g], jnp.zeros((HEAD_SIZE - few, rows), jnp.float32)], axis=0
+                ).T
+                for h in range(per_group):
+                    part = pl.ds(h * rows, rows)
+                    there = stats[:, h : h + 1]
+                    here = m[g, part, :]
+                    new_m = jnp.maximum(here, there)
+                    fade = jnp.exp2((here - new_m) * SCALE)
+                    weight = jnp.exp2((there - new_m) * SCALE) * stats[:, per_group + h : per_group + h + 1]
+                    top = acc[g, part, :HEAD_SIZE] * fade + back[g, part, :].astype(jnp.float32) * weight
+                    low = acc[g, part, HEAD_SIZE:] * fade + weight
+                    at = pl.multiple_of((g * per_group + h) * HEAD_SIZE, HEAD_SIZE)
+                    o[0, :, pl.ds(at, HEAD_SIZE)] = (top / low).astype(jnp.bfloat16)
+
+    for p in range(2):
+        away = moved_heads(n, groups, p)
+
+        @pl.when((me < last) & (phase == p))
+        def _(away=away):
+            @pl.loop(0, me + 1)
+            def _(slot):
+                for g in range(groups):
+                    if g < away:
+                        @pl.when(me < helper)
+                        def _():
+                            send(slot, g).wait_send()
+                    else:
+                        send(slot, g).wait_send()
+
+        for g in range(away):
+            @pl.when((me == last) & (phase == p))
+            def _(g=g):
+                ask(g).wait_send()
+
+            @pl.when((me == helper) & (phase == p))
+            def _(g=g):
+                for copy in give(g):
+                    copy.wait_send()
+
+
+def scheduled(n, queries, keys, values):
+    rows, query_width = queries.shape[1:]
+    groups = keys.shape[2] // HEAD_SIZE
+    per_group = query_width // HEAD_SIZE // groups
+    tall = per_group * rows
+    most = max(moved_heads(n, groups, p) for p in range(2))
+    held = max(most, 1)
+    few = -(-2 * per_group // 8) * 8
+    hbm = pl.BlockSpec(memory_space=pltpu.HBM)
+    total = groups + most
+    bytes_held = (
+        2 * rows * query_width * 2
+        + total * tall * HEAD_SIZE * (2 + 4 + 8)
+        + 2 * n * rows * keys.shape[2] * 2
+        + 2 * held * (tall * HEAD_SIZE * 2 + few * rows * 4)
+    )
+    return pl.pallas_call(
+        functools.partial(scheduled_kernel, n, groups, per_group, most),
+        out_shape=jax.ShapeDtypeStruct(queries.shape, queries.dtype),
+        in_specs=[hbm, hbm, hbm],
+        out_specs=pl.BlockSpec(memory_space=pltpu.VMEM),
+        scratch_shapes=[
+            pltpu.VMEM((total, tall, HEAD_SIZE), jnp.bfloat16),
+            pltpu.VMEM((n, groups, 2 * rows, HEAD_SIZE), jnp.bfloat16),
+            pltpu.VMEM((total, tall, HEAD_SIZE), jnp.float32),
+            pltpu.VMEM((total, tall, 2 * HEAD_SIZE), jnp.float32),
+            pltpu.VMEM((held, tall, HEAD_SIZE), jnp.bfloat16),
+            pltpu.VMEM((held, few, rows), jnp.float32),
+            pltpu.VMEM((held, tall, HEAD_SIZE), jnp.bfloat16),
+            pltpu.VMEM((held, few, rows), jnp.float32),
+            pltpu.SemaphoreType.DMA((2, groups)),
+            pltpu.SemaphoreType.DMA((groups, per_group)),
+            pltpu.SemaphoreType.DMA((n, groups)),
+            pltpu.SemaphoreType.DMA((n, groups)),
+            pltpu.SemaphoreType.DMA((held,)),
+            pltpu.SemaphoreType.DMA((held,)),
+            pltpu.SemaphoreType.DMA((2, held)),
+            pltpu.SemaphoreType.DMA((2, held)),
+        ],
+        compiler_params=pltpu.CompilerParams(
+            collective_id=0, has_side_effects=True, vmem_limit_bytes=bytes_held + 4 * 2**20
+        ),
+    )(*(pltpu.with_memory_space_constraint(x, pltpu.HBM) for x in (queries, keys, values)))
 
 
 def kernel(
@@ -182,8 +618,9 @@
 
 def solution(mesh):
     spec = P(("groups", "batch"), "seq", None)
+    n = mesh.shape["seq"]
     return jax.shard_map(
-        functools.partial(on_device, mesh.shape["seq"]),
+        functools.partial(scheduled if n <= SCHEDULED else on_device, n),
         mesh=mesh,
         in_specs=(spec, spec, spec),
         out_specs=spec,

time: 21.2 us -> 20.5 us (0.967)
  the two profiles are of different devices: /device:TPU:24 before, /device:TPU:31 now
where the time goes in v1:
time: 20.5 us; the launch traced here: 20.3 us
  Pallas kernels  19.5 us (95%)
  local copies, waits for them, and re-layouts  0.8 us (4%)
    pallas_call x1, Pallas kernels, scheduled(): pl.pallas_call(functools.partial(scheduled_kernel, n, groups, per_group,...  19.5 us
    unnamed x1, local copies, waits for them, and re-layouts  0.8 us

profile of v1, /device:TPU:31, one launch (start us, length us, event | category | flops | bytes accessed | tf_op | source)
XLA Modules:
  0.0 20.3 jit_solution(5630415996336759753)
XLA Ops:
  0.0 19.5 %shard_map.37 = bf16[1,128,2048]{2,1,0:T(8,128)(2,1)S(1)} custom-call(bf16[1,128,2048]{2,1,0:T(8,128)(2,1)} %q_hbm.1, bf16[1,128,512]{2,1,0:T(8,128)(2,1)} %k_hbm.1, bf16[1,128,512]{2,1,0:T(8,128)(2,1)} %v_hbm.1), custom_call_target="tpu_custom_call" | custom-call | tf_op jit(solution)/shard_map/pallas_call | solution.py:423
  19.5 0.8 %copy.5 = bf16[1,128,2048]{2,1,0:T(8,128)(2,1)} copy(bf16[1,128,2048]{2,1,0:T(8,128)(2,1)S(1)} %shard_map.37) | data formatting | bytes 1048576

commit v2 on v1

--- a/solution.py
+++ b/solution.py
@@ -119,11 +119,12 @@
 def scheduled_kernel(
     n, groups, per_group, most,
     q_hbm, k_hbm, v_hbm, o,
-    q, kv, m, acc, back, back_stats, mine, mine_stats,
+    q, qt, kv, m, l, acc, back, back_stats, mine, mine_stats,
     load_sem, q_sem, send_sem, recv_sem, ask_send, ask_recv, back_send, back_recv,
 ):
     rows = kv.shape[2] // 2
-    tall = per_group * rows
+    tall = per_group * HEAD_SIZE
+    wide = per_group * rows
     me = lax.axis_index("seq")
     phase = lax.rem(lax.axis_index("batch"), 2)
     last, helper = n - 1, n - 2
@@ -139,12 +140,9 @@
             ),
         )
 
-    def q_load(g, h):
-        return pltpu.make_async_copy(
-            q_hbm.at[0, :, pl.ds((g * per_group + h) * HEAD_SIZE, HEAD_SIZE)],
-            q.at[g, pl.ds(h * rows, rows)],
-            q_sem.at[g, h],
-        )
+    def q_load(g):
+        cols = pl.ds(g * tall, tall)
+        return pltpu.make_async_copy(q_hbm.at[0, :, cols], q.at[g], q_sem.at[g])
 
     def send(slot, g):
         return pltpu.make_async_remote_copy(
@@ -211,8 +209,7 @@
         for copy in kv_load(g):
             copy.start()
     for g in range(groups):
-        for h in range(per_group):
-            q_load(g, h).start()
+        q_load(g).start()
 
     scripts = {(r, p): script(n, groups, p, r) for r in range(n) for p in range(2)}
     here = {key: (me == key[0]) & (phase == key[1]) for key in scripts}
@@ -242,8 +239,7 @@
         def _(rank=rank, p=p, before=before):
             if rank == last:
                 for g in range(moved_heads(n, groups, p)):
-                    for h in range(per_group):
-                        q_load(g, h).wait()
+                    q_load(g).wait()
                     ask(g).start()
             for g in before:
                 for copy in kv_load(g):
@@ -255,51 +251,38 @@
                         copy.wait()
             for g in range(groups):
                 if rank < last or g >= moved_heads(n, groups, p):
-                    for h in range(per_group):
-                        q_load(g, h).wait()
-
-    def scores_of(slot, g, qi):
-        return lax.dot_general(
-            q[qi],
-            kv[slot, g, :rows, :],
-            (((1,), (1,)), ((), ())),
-            preferred_element_type=jnp.float32,
-        )
+                    q_load(g).wait()
+
+    def scores_of(slot, g, turned):
+        return jnp.dot(kv[slot, g, :rows, :], turned, preferred_element_type=jnp.float32)
 
     def weighted(p, slot, g):
-        block = jnp.concatenate(
-            [kv[slot, g, rows:, :], jnp.ones((rows, HEAD_SIZE), jnp.bfloat16)], axis=1
-        )
-        return jnp.dot(p.astype(jnp.bfloat16), block, preferred_element_type=jnp.float32)
+        return jnp.dot(
+            kv[slot, g, rows:, :].T, p.astype(jnp.bfloat16), preferred_element_type=jnp.float32
+        )
 
     def write(total, g):
-        done = (total[:, :HEAD_SIZE] / total[:, HEAD_SIZE:]).astype(jnp.bfloat16)
+        done = total.astype(jnp.bfloat16)
         for h in range(per_group):
             at = pl.multiple_of((g * per_group + h) * HEAD_SIZE, HEAD_SIZE)
-            o[0, :, pl.ds(at, HEAD_SIZE)] = done[h * rows : (h + 1) * rows]
+            o[0, :, pl.ds(at, HEAD_SIZE)] = done[:, h * rows : (h + 1) * rows].T
 
     def conclude(qi, g, flag):
         @pl.when(flag == FINISH)
         def _():
-            write(acc[qi], g)
+            write(acc[qi] / l[qi], g)
 
         if most:
             @pl.when(flag == RETURN)
             def _():
-                total = acc[qi]
-                mine[g] = (total[:, :HEAD_SIZE] / total[:, HEAD_SIZE:]).astype(jnp.bfloat16)
-                lane = lax.broadcasted_iota(jnp.int32, (rows, HEAD_SIZE), 1)
-                stats = jnp.zeros((rows, HEAD_SIZE), jnp.float32)
-                for h in range(per_group):
-                    part = pl.ds(h * rows, rows)
-                    stats = jnp.where(lane == h, m[qi, part, :], stats)
-                    stats = jnp.where(lane == per_group + h, acc[qi, part, HEAD_SIZE:], stats)
-                mine_stats[g] = stats.T[: mine_stats.shape[1]]
+                mine[g] = (acc[qi] / l[qi]).astype(jnp.bfloat16)
+                mine_stats[g, 0:1] = m[qi]
+                mine_stats[g, 1:2] = l[qi]
                 for copy in give(g):
                     copy.start()
 
-    row = lax.rem(lax.broadcasted_iota(jnp.int32, (tall, rows), 0), rows)
-    column = lax.broadcasted_iota(jnp.int32, (tall, rows), 1)
+    key = lax.broadcasted_iota(jnp.int32, (rows, wide), 0)
+    query = lax.rem(lax.broadcasted_iota(jnp.int32, (rows, wide), 1), rows)
 
     @pl.loop(0, groups + count)
     def _(i):
@@ -339,22 +322,26 @@
 
         @pl.when(op == FIRST)
         def _():
-            ahead = rows * answer
-            s = jnp.where(column <= row + ahead, scores_of(0, g, qi), -1e30)
-            new_m = jnp.max(s, axis=1, keepdims=True)
-            acc[qi] = weighted(jnp.exp2((s - new_m) * SCALE), 0, g)
-            m[qi] = jnp.broadcast_to(new_m, m.shape[1:])
+            for h in range(per_group):
+                qt[qi, :, h * rows : (h + 1) * rows] = q[qi, :, h * HEAD_SIZE : (h + 1) * HEAD_SIZE].T
+            s = jnp.where(key <= query + rows * answer, scores_of(0, g, qt[qi]), -1e30)
+            new_m = jnp.max(s, axis=0, keepdims=True)
+            p = jnp.exp2((s - new_m) * SCALE)
+            m[qi] = new_m
+            l[qi] = jnp.sum(p, axis=0, keepdims=True)
+            acc[qi] = weighted(p, 0, g)
             conclude(qi, g, flag)
 
         @pl.when(op == NEXT)
         def _():
-            s = scores_of(slot, g, qi)
+            s = scores_of(slot, g, qt[qi])
             old_m = m[qi]
-            new_m = jnp.maximum(old_m, jnp.max(s, axis=1, keepdims=True))
+            new_m = jnp.maximum(old_m, jnp.max(s, axis=0, keepdims=True))
             fade = jnp.exp2((old_m - new_m) * SCALE)
-            p = jnp.exp2((s - new_m[:, :1]) * SCALE)
-            acc[qi] = acc[qi] * jnp.concatenate([fade, fade], axis=1) + weighted(p, slot, g)
+            p = jnp.exp2((s - new_m) * SCALE)
             m[qi] = new_m
+            l[qi] = l[qi] * fade + jnp.sum(p, axis=0, keepdims=True)
+            acc[qi] = acc[qi] * fade + weighted(p, slot, g)
             conclude(qi, g, flag)
 
         if most:
@@ -362,21 +349,12 @@
             def _():
                 for copy in give(g):
                     copy.wait_recv()
-                few = back_stats.shape[1]
-                stats = jnp.concatenate(
-                    [back_stats[g], jnp.zeros((HEAD_SIZE - few, rows), jnp.float32)], axis=0
-                ).T
-                for h in range(per_group):
-                    part = pl.ds(h * rows, rows)
-                    there = stats[:, h : h + 1]
-                    here = m[g, part, :]
-                    new_m = jnp.maximum(here, there)
-                    fade = jnp.exp2((here - new_m) * SCALE)
-                    weight = jnp.exp2((there - new_m) * SCALE) * stats[:, per_group + h : per_group + h + 1]
-                    top = acc[g, part, :HEAD_SIZE] * fade + back[g, part, :].astype(jnp.float32) * weight
-                    low = acc[g, part, HEAD_SIZE:] * fade + weight
-                    at = pl.multiple_of((g * per_group + h) * HEAD_SIZE, HEAD_SIZE)
-                    o[0, :, pl.ds(at, HEAD_SIZE)] = (top / low).astype(jnp.bfloat16)
+                here, there = m[g], back_stats[g, 0:1]
+                new_m = jnp.maximum(here, there)
+                fade = jnp.exp2((here - new_m) * SCALE)
+                weight = jnp.exp2((there - new_m) * SCALE) * back_stats[g, 1:2]
+                total = acc[g] * fade + back[g].astype(jnp.float32) * weight
+                write(total / (l[g] * fade + weight), g)
 
     for p in range(2):
         away = moved_heads(n, groups, p)
@@ -408,17 +386,17 @@
     rows, query_width = queries.shape[1:]
     groups = keys.shape[2] // HEAD_SIZE
     per_group = query_width // HEAD_SIZE // groups
-    tall = per_group * rows
+    tall, wide = per_group * HEAD_SIZE, per_group * rows
     most = max(moved_heads(n, groups, p) for p in range(2))
     held = max(most, 1)
-    few = -(-2 * per_group // 8) * 8
     hbm = pl.BlockSpec(memory_space=pltpu.HBM)
     total = groups + most
     bytes_held = (
         2 * rows * query_width * 2
-        + total * tall * HEAD_SIZE * (2 + 4 + 8)
+        + total * rows * tall * (2 + 2 + 4)
         + 2 * n * rows * keys.shape[2] * 2
-        + 2 * held * (tall * HEAD_SIZE * 2 + few * rows * 4)
+        + 2 * held * rows * tall * 2
+        + (2 * total + 4 * held) * 8 * wide * 4
     )
     return pl.pallas_call(
         functools.partial(scheduled_kernel, n, groups, per_group, most),
@@ -426,16 +404,18 @@
         in_specs=[hbm, hbm, hbm],
         out_specs=pl.BlockSpec(memory_space=pltpu.VMEM),
         scratch_shapes=[
-            pltpu.VMEM((total, tall, HEAD_SIZE), jnp.bfloat16),
+            pltpu.VMEM((total, rows, tall), jnp.bfloat16),
+            pltpu.VMEM((total, HEAD_SIZE, wide), jnp.bfloat16),
             pltpu.VMEM((n, groups, 2 * rows, HEAD_SIZE), jnp.bfloat16),
-            pltpu.VMEM((total, tall, HEAD_SIZE), jnp.float32),
-            pltpu.VMEM((total, tall, 2 * HEAD_SIZE), jnp.float32),
-            pltpu.VMEM((held, tall, HEAD_SIZE), jnp.bfloat16),
-            pltpu.VMEM((held, few, rows), jnp.float32),
-            pltpu.VMEM((held, tall, HEAD_SIZE), jnp.bfloat16),
-            pltpu.VMEM((held, few, rows), jnp.float32),
+            pltpu.VMEM((total, 1, wide), jnp.float32),
+            pltpu.VMEM((total, 1, wide), jnp.float32),
+            pltpu.VMEM((total, HEAD_SIZE, wide), jnp.float32),
+            pltpu.VMEM((held, HEAD_SIZE, wide), jnp.bfloat16),
+            pltpu.VMEM((held, 2, wide), jnp.float32),
+            pltpu.VMEM((held, HEAD_SIZE, wide), jnp.bfloat16),
+            pltpu.VMEM((held, 2, wide), jnp.float32),
             pltpu.SemaphoreType.DMA((2, groups)),
-            pltpu.SemaphoreType.DMA((groups, per_group)),
+            pltpu.SemaphoreType.DMA((groups,)),
             pltpu.SemaphoreType.DMA((n, groups)),
             pltpu.SemaphoreType.DMA((n, groups)),
             pltpu.SemaphoreType.DMA((held,)),

time: 20.5 us -> 19.7 us (0.961)
  the two profiles are of different devices: /device:TPU:31 before, /device:TPU:25 now
where the time goes in v2:
time: 19.7 us; the launch traced here: 19.5 us
  Pallas kernels  18.7 us (95%)
  local copies, waits for them, and re-layouts  0.8 us (4%)
    pallas_call x1, Pallas kernels, scheduled(): pl.pallas_call(functools.partial(scheduled_kernel, n, groups, per_group,...  18.7 us
    unnamed x1, local copies, waits for them, and re-layouts  0.8 us

profile of v2, /device:TPU:25, one launch (start us, length us, event | category | flops | bytes accessed | tf_op | source)
XLA Modules:
  0.0 19.5 jit_solution(18347713001611623066)
XLA Ops:
  0.0 18.7 %shard_map.37 = bf16[1,128,2048]{2,1,0:T(8,128)(2,1)S(1)} custom-call(bf16[1,128,2048]{2,1,0:T(8,128)(2,1)} %q_hbm.1, bf16[1,128,512]{2,1,0:T(8,128)(2,1)} %k_hbm.1, bf16[1,128,512]{2,1,0:T(8,128)(2,1)} %v_hbm.1), custom_call_target="tpu_custom_call" | custom-call | tf_op jit(solution)/shard_map/pallas_call | solution.py:401
  18.7 0.8 %copy.5 = bf16[1,128,2048]{2,1,0:T(8,128)(2,1)} copy(bf16[1,128,2048]{2,1,0:T(8,128)(2,1)S(1)} %shard_map.37) | data formatting | bytes 1048576

commit v3 on v2

--- a/solution.py
+++ b/solution.py
@@ -14,7 +14,7 @@
 
 SCHEDULED = 4
 
-FIRST, NEXT, MERGE = range(3)
+FIRST, NEXT, MERGE, REST = range(4)
 KEEP, FINISH, RETURN = range(3)
 CODE = 2**14
 
@@ -86,7 +86,10 @@
         if queue and queue[0] == (b, g):
             queue.pop(0)
             how["forward"] = 1
-            if queue and queue[0][0] == rank:
+            while queue and queue[0][0] == rank:
+                if "then" in how:
+                    steps.append(pack(REST, slot, g, **how))
+                    how = {}
                 how["then"] = queue.pop(0)[1] + 1
         left[g] -= 1
         if g in waiting:
@@ -108,7 +111,7 @@
     if rank == last:
         steps += [pack(MERGE, 0, g) for g in range(returned, moved)]
     assert not queue
-    return before, steps
+    return before, steps, len(arrivals)
 
 
 def returns_before(order, moved, g, groups):
@@ -120,7 +123,7 @@
     n, groups, per_group, most,
     q_hbm, k_hbm, v_hbm, o,
     q, qt, kv, m, l, acc, back, back_stats, mine, mine_stats,
-    load_sem, q_sem, send_sem, recv_sem, ask_send, ask_recv, back_send, back_recv,
+    load_sem, send_sem, aside_sem, recv_sem, stats_sem,
 ):
     rows = kv.shape[2] // 2
     tall = per_group * HEAD_SIZE
@@ -133,43 +136,45 @@
         cols = pl.ds(g * HEAD_SIZE, HEAD_SIZE)
         return (
             pltpu.make_async_copy(
-                k_hbm.at[0, :, cols], kv.at[0, g, pl.ds(0, rows)], load_sem.at[0, g]
+                k_hbm.at[0, :, cols], kv.at[0, g, pl.ds(0, rows)], load_sem.at[0]
             ),
             pltpu.make_async_copy(
-                v_hbm.at[0, :, cols], kv.at[0, g, pl.ds(rows, rows)], load_sem.at[1, g]
+                v_hbm.at[0, :, cols], kv.at[0, g, pl.ds(rows, rows)], load_sem.at[0]
             ),
         )
 
     def q_load(g):
         cols = pl.ds(g * tall, tall)
-        return pltpu.make_async_copy(q_hbm.at[0, :, cols], q.at[g], q_sem.at[g])
-
-    def send(slot, g):
+        return pltpu.make_async_copy(q_hbm.at[0, :, cols], q.at[g], load_sem.at[1])
+
+    scripts = {(r, p): script(n, groups, p, r) for r in range(n) for p in range(2)}
+    here = {key: (me == key[0]) & (phase == key[1]) for key in scripts}
+
+    def wait_for(ref, sem):
+        pltpu.make_async_copy(ref, ref, sem).wait()
+
+    def send(slot, g, nth):
         return pltpu.make_async_remote_copy(
             src_ref=kv.at[slot, g],
             dst_ref=kv.at[slot + 1, g],
-            send_sem=send_sem.at[slot, g],
-            recv_sem=recv_sem.at[slot + 1, g],
+            send_sem=send_sem.at[0],
+            recv_sem=recv_sem.at[nth],
             device_id={"seq": jnp.minimum(me + 1, last)},
             device_id_type=MESH,
         )
 
-    def receive(slot, g):
-        return pltpu.make_async_remote_copy(
-            src_ref=kv.at[slot, g],
-            dst_ref=kv.at[slot, g],
-            send_sem=send_sem.at[slot, g],
-            recv_sem=recv_sem.at[slot, g],
-            device_id={"seq": jnp.minimum(me + 1, last)},
-            device_id_type=MESH,
-        )
+    def arrived(ref, nth):
+        pltpu.make_async_copy(ref, ref, recv_sem.at[nth]).wait()
+
+    asked_at = scripts[helper, 0][2]
+    given_at = jnp.where(phase == 0, scripts[last, 0][2], scripts[last, 1][2])
 
     def ask(g):
         return pltpu.make_async_remote_copy(
             src_ref=q.at[g],
             dst_ref=q.at[groups + g],
-            send_sem=ask_send.at[g],
-            recv_sem=ask_recv.at[g],
+            send_sem=aside_sem.at[0],
+            recv_sem=recv_sem.at[asked_at + g],
             device_id={"seq": jnp.int32(helper)},
             device_id_type=MESH,
         )
@@ -179,16 +184,16 @@
             pltpu.make_async_remote_copy(
                 src_ref=mine.at[g],
                 dst_ref=back.at[g],
-                send_sem=back_send.at[0, g],
-                recv_sem=back_recv.at[0, g],
+                send_sem=aside_sem.at[0],
+                recv_sem=recv_sem.at[given_at + g],
                 device_id={"seq": jnp.int32(last)},
                 device_id_type=MESH,
             ),
             pltpu.make_async_remote_copy(
                 src_ref=mine_stats.at[g],
                 dst_ref=back_stats.at[g],
-                send_sem=back_send.at[1, g],
-                recv_sem=back_recv.at[1, g],
+                send_sem=aside_sem.at[1],
+                recv_sem=stats_sem.at[g],
                 device_id={"seq": jnp.int32(last)},
                 device_id_type=MESH,
             ),
@@ -210,9 +215,6 @@
             copy.start()
     for g in range(groups):
         q_load(g).start()
-
-    scripts = {(r, p): script(n, groups, p, r) for r in range(n) for p in range(2)}
-    here = {key: (me == key[0]) & (phase == key[1]) for key in scripts}
 
     def pick(values):
         out = jnp.int32(0)
@@ -221,37 +223,34 @@
                 out = jnp.where(here[key], jnp.int32(value), out)
         return out
 
-    count = pick({key: len(steps) for key, (_, steps) in scripts.items()})
-    longest = max(len(steps) for _, steps in scripts.values())
+    count = pick({key: len(steps) for key, (_, steps, _) in scripts.items()})
+    longest = max(len(steps) for _, steps, _ in scripts.values())
     words = []
     for at in range(0, longest, 2):
-        pairs = {key: (steps[at : at + 2] + [0, 0])[:2] for key, (_, steps) in scripts.items()}
+        pairs = {key: (steps[at : at + 2] + [0, 0])[:2] for key, (_, steps, _) in scripts.items()}
         words.append(pick({key: low + CODE * high for key, (low, high) in pairs.items()}))
 
     @pl.when(me < last if not most else me >= 0)
     def _():
         pl.semaphore_wait(barrier, 1)
 
-    for key, (before, _) in scripts.items():
-        rank, p = key
-
-        @pl.when(here[key])
-        def _(rank=rank, p=p, before=before):
-            if rank == last:
-                for g in range(moved_heads(n, groups, p)):
-                    q_load(g).wait()
-                    ask(g).start()
-            for g in before:
-                for copy in kv_load(g):
-                    copy.wait()
-                send(0, g).start()
-            for g in range(groups):
-                if g not in before:
-                    for copy in kv_load(g):
-                        copy.wait()
-            for g in range(groups):
-                if rank < last or g >= moved_heads(n, groups, p):
-                    q_load(g).wait()
+    wait_for(kv.at[0], load_sem.at[0])
+
+    for (rank, p), (before, _, _) in scripts.items():
+        @pl.when(here[rank, p])
+        def _(before=before):
+            for i, g in enumerate(before):
+                send(0, g, i).start()
+
+    wait_for(q.at[pl.ds(0, groups)], load_sem.at[1])
+
+    for p in range(2):
+        for g in range(moved_heads(n, groups, p)):
+            @pl.when(here[last, p])
+            def _(g=g):
+                ask(g).start()
+
+    sent_before = pick({key: len(before) for key, (before, _, _) in scripts.items()})
 
     def scores_of(slot, g, turned):
         return jnp.dot(kv[slot, g, :rows, :], turned, preferred_element_type=jnp.float32)
@@ -270,12 +269,12 @@
     def conclude(qi, g, flag):
         @pl.when(flag == FINISH)
         def _():
-            write(acc[qi] / l[qi], g)
+            write(acc[qi] * (1.0 / l[qi]), g)
 
         if most:
             @pl.when(flag == RETURN)
             def _():
-                mine[g] = (acc[qi] / l[qi]).astype(jnp.bfloat16)
+                mine[g] = (acc[qi] * (1.0 / l[qi])).astype(jnp.bfloat16)
                 mine_stats[g, 0:1] = m[qi]
                 mine_stats[g, 1:2] = l[qi]
                 for copy in give(g):
@@ -284,8 +283,8 @@
     key = lax.broadcasted_iota(jnp.int32, (rows, wide), 0)
     query = lax.rem(lax.broadcasted_iota(jnp.int32, (rows, wide), 1), rows)
 
-    @pl.loop(0, groups + count)
-    def _(i):
+    def step(i, counts):
+        got, sent = counts
         at = jnp.maximum(i - groups, 0)
         word = words[0] if words else jnp.int32(0)
         for j, other in enumerate(words[1:]):
@@ -305,20 +304,22 @@
 
         @pl.when(wait == 1)
         def _():
-            receive(slot, g).wait_recv()
+            arrived(kv.at[slot, g], got)
 
             @pl.when(forward == 1)
             def _():
-                send(slot, g).start()
-
-            @pl.when(then > 0)
-            def _():
-                send(0, then - 1).start()
+                send(slot, g, sent).start()
+
+        sent = sent + forward
+
+        @pl.when(then > 0)
+        def _():
+            send(0, then - 1, sent).start()
 
         if most:
             @pl.when((op == FIRST) & (answer == 1))
             def _():
-                ask(g).wait_recv()
+                arrived(q.at[groups + g], asked_at + g)
 
         @pl.when(op == FIRST)
         def _():
@@ -347,39 +348,33 @@
         if most:
             @pl.when(op == MERGE)
             def _():
-                for copy in give(g):
-                    copy.wait_recv()
+                arrived(back.at[g], given_at + g)
+                wait_for(back_stats.at[g], stats_sem.at[g])
                 here, there = m[g], back_stats[g, 0:1]
                 new_m = jnp.maximum(here, there)
                 fade = jnp.exp2((here - new_m) * SCALE)
                 weight = jnp.exp2((there - new_m) * SCALE) * back_stats[g, 1:2]
-                total = acc[g] * fade + back[g].astype(jnp.float32) * weight
-                write(total / (l[g] * fade + weight), g)
-
-    for p in range(2):
+                share = 1.0 / (l[g] * fade + weight)
+                write(acc[g] * (fade * share) + back[g].astype(jnp.float32) * (weight * share), g)
+
+        return got + wait, sent + jnp.where(then > 0, 1, 0)
+
+    lax.fori_loop(0, groups + count, step, (jnp.int32(0), sent_before))
+
+    for (rank, p) in scripts:
         away = moved_heads(n, groups, p)
 
-        @pl.when((me < last) & (phase == p))
-        def _(away=away):
-            @pl.loop(0, me + 1)
-            def _(slot):
-                for g in range(groups):
-                    if g < away:
-                        @pl.when(me < helper)
-                        def _():
-                            send(slot, g).wait_send()
-                    else:
-                        send(slot, g).wait_send()
-
-        for g in range(away):
-            @pl.when((me == last) & (phase == p))
-            def _(g=g):
-                ask(g).wait_send()
-
-            @pl.when((me == helper) & (phase == p))
-            def _(g=g):
-                for copy in give(g):
-                    copy.wait_send()
+        @pl.when(here[rank, p])
+        def _(rank=rank, away=away):
+            if rank < helper:
+                wait_for(kv.at[pl.ds(0, rank + 1)], send_sem.at[0])
+            elif rank == helper:
+                wait_for(kv.at[pl.ds(0, rank + 1), pl.ds(away, groups - away)], send_sem.at[0])
+                if away:
+                    wait_for(mine.at[pl.ds(0, away)], aside_sem.at[0])
+                    wait_for(mine_stats.at[pl.ds(0, away)], aside_sem.at[1])
+            elif away:
+                wait_for(q.at[pl.ds(0, away)], aside_sem.at[0])
 
 
 def scheduled(n, queries, keys, values):
@@ -391,6 +386,11 @@
     held = max(most, 1)
     hbm = pl.BlockSpec(memory_space=pltpu.HBM)
     total = groups + most
+    received = max(
+        script(n, groups, p, r)[2] + (moved_heads(n, groups, p) if r >= n - 2 else 0)
+        for p in range(2)
+        for r in range(n)
+    )
     bytes_held = (
         2 * rows * query_width * 2
         + total * rows * tall * (2 + 2 + 4)
@@ -414,14 +414,11 @@
             pltpu.VMEM((held, 2, wide), jnp.float32),
             pltpu.VMEM((held, HEAD_SIZE, wide), jnp.bfloat16),
             pltpu.VMEM((held, 2, wide), jnp.float32),
-            pltpu.SemaphoreType.DMA((2, groups)),
-            pltpu.SemaphoreType.DMA((groups,)),
-            pltpu.SemaphoreType.DMA((n, groups)),
-            pltpu.SemaphoreType.DMA((n, groups)),
+            pltpu.SemaphoreType.DMA((2,)),
+            pltpu.SemaphoreType.DMA((1,)),
+            pltpu.SemaphoreType.DMA((2,)),
+            pltpu.SemaphoreType.DMA((received,)),
             pltpu.SemaphoreType.DMA((held,)),
-            pltpu.SemaphoreType.DMA((held,)),
-            pltpu.SemaphoreType.DMA((2, held)),
-            pltpu.SemaphoreType.DMA((2, held)),
         ],
         compiler_params=pltpu.CompilerParams(
             collective_id=0, has_side_effects=True, vmem_limit_bytes=bytes_held + 4 * 2**20

time: 19.7 us -> 19.3 us (0.980)
  Pallas kernels: 18.7 us -> 18.4 us
    pallas_call x1, Pallas kernels: 18.7 us -> 18.4 us  [scheduled(): pl.pallas_call(functools.partial(scheduled_kernel, n, groups, per_group,...]
where the time goes in v3:
time: 19.3 us; the launch traced here: 19.2 us
  Pallas kernels  18.4 us (95%)
  local copies, waits for them, and re-layouts  0.8 us (4%)
    pallas_call x1, Pallas kernels, scheduled(): pl.pallas_call(functools.partial(scheduled_kernel, n, groups, per_group,...  18.4 us
    unnamed x1, local copies, waits for them, and re-layouts  0.8 us

profile of v3, /device:TPU:25, one launch (start us, length us, event | category | flops | bytes accessed | tf_op | source)
XLA Modules:
  0.0 19.2 jit_solution(15016506789582225401)
XLA Ops:
  0.0 18.4 %shard_map.37 = bf16[1,128,2048]{2,1,0:T(8,128)(2,1)S(1)} custom-call(bf16[1,128,2048]{2,1,0:T(8,128)(2,1)} %q_hbm.1, bf16[1,128,512]{2,1,0:T(8,128)(2,1)} %k_hbm.1, bf16[1,128,512]{2,1,0:T(8,128)(2,1)} %v_hbm.1), custom_call_target="tpu_custom_call" | custom-call | tf_op jit(solution)/shard_map/pallas_call | solution.py:401
  18.4 0.8 %copy.5 = bf16[1,128,2048]{2,1,0:T(8,128)(2,1)} copy(bf16[1,128,2048]{2,1,0:T(8,128)(2,1)S(1)} %shard_map.37) | data formatting | bytes 1048576

commit v4 on v3

--- a/solution.py
+++ b/solution.py
@@ -47,6 +47,10 @@
     for g in range(moved):
         out += [(b, g) for b in [*older, top]]
     return out
+
+
+def taken_up(phase, g):
+    return 2 if phase else 2 + 2 * g
 
 
 def script(n, groups, phase, rank):
@@ -100,9 +104,9 @@
             seen[g].append(slot)
         ends = left[g] == 0 and not (rank == last and g < moved)
         steps.append(pack(NEXT, slot, g, flag=FINISH if ends else KEEP, **how))
-        if i + 1 < len(arrivals):
-            h = arrivals[i + 1][1]
-            if h in waiting and waiting[h] == 1:
+        for h in waiting:
+            due = i + 1 < len(arrivals) and arrivals[i + 1][1] == h and waiting[h] == 1
+            if h not in ready and (due or i >= taken_up(phase, h)):
                 start_answer(h)
         if rank == last:
             while returned < moved and returns_before(order, moved, returned, groups) <= i + 1:

time: 19.3 us -> 19.2 us (level)
  no operation moved by 1% of the time
where the time goes in v4:
time: 19.2 us; the launch traced here: 19.1 us
  Pallas kernels  18.3 us (95%)
  local copies, waits for them, and re-layouts  0.8 us (4%)
    pallas_call x1, Pallas kernels, scheduled(): pl.pallas_call(functools.partial(scheduled_kernel, n, groups, per_group,...  18.3 us
    unnamed x1, local copies, waits for them, and re-layouts  0.8 us

profile of v4, /device:TPU:25, one launch (start us, length us, event | category | flops | bytes accessed | tf_op | source)
XLA Modules:
  0.0 19.1 jit_solution(16297708706434134795)
XLA Ops:
  0.0 18.3 %shard_map.37 = bf16[1,128,2048]{2,1,0:T(8,128)(2,1)S(1)} custom-call(bf16[1,128,2048]{2,1,0:T(8,128)(2,1)} %q_hbm.1, bf16[1,128,512]{2,1,0:T(8,128)(2,1)} %k_hbm.1, bf16[1,128,512]{2,1,0:T(8,128)(2,1)} %v_hbm.1), custom_call_target="tpu_custom_call" | custom-call | tf_op jit(solution)/shard_map/pallas_call | solution.py:405
  18.3 0.8 %copy.5 = bf16[1,128,2048]{2,1,0:T(8,128)(2,1)} copy(bf16[1,128,2048]{2,1,0:T(8,128)(2,1)S(1)} %shard_map.37) | data formatting | bytes 1048576

commit v5 on v4

--- a/solution.py
+++ b/solution.py
@@ -27,30 +27,19 @@
 
 
 def moved_heads(n, groups, phase):
-    return 0 if n < 4 else groups // (2 if phase == 0 else 4)
+    return 0 if n < 4 else groups // (4 if phase == 0 else 2)
 
 
 def order_of(top, groups, moved, phase):
     stay = list(range(moved, groups))
-    older = range(top - 1, -1, -1)
-    if phase == 0 and moved:
-        out = [(top, 0)] + [(top, g) for g in stay] + [(b, 0) for b in older]
-        for g in range(1, moved):
-            out += [(b, g) for b in range(top, -1, -1)]
-        return out + [(b, g) for b in older for g in stay]
-    ahead = [(top, g) for g in stay[1:]]
-    out = [(top, stay[0])]
-    behind = [(b, g) for b in older for g in stay[1:] + stay[:1]]
-    for i, unit in enumerate(behind):
-        out += [unit] + (ahead[i - 1 : i] if 0 < i else [])
-    out += ahead[max(len(behind) - 1, 0) :]
-    for g in range(moved):
-        out += [(b, g) for b in [*older, top]]
-    return out
+    own = [(top, g) for g in stay]
+    older = [(b, g) for b in range(top - 1, -1, -1) for g in stay]
+    away = [(b, g) for g in range(moved) for b in range(top, -1, -1)]
+    return own + older + away if phase == 0 else own + away + older
 
 
 def taken_up(phase, g):
-    return 2 if phase else 2 + 2 * g
+    return 2 + 2 * g
 
 
 def script(n, groups, phase, rank):

time: 19.2 us -> 19 us (0.990)
  the two profiles are of different devices: /device:TPU:25 before, /device:TPU:24 now
where the time goes in v5:
time: 19 us; the launch traced here: 18.8 us
  Pallas kernels  18 us (95%)
  local copies, waits for them, and re-layouts  0.8 us (4%)
    pallas_call x1, Pallas kernels, scheduled(): pl.pallas_call(functools.partial(scheduled_kernel, n, groups, per_group,...  18 us
    unnamed x1, local copies, waits for them, and re-layouts  0.8 us

profile of v5, /device:TPU:24, one launch (start us, length us, event | category | flops | bytes accessed | tf_op | source)
XLA Modules:
  0.0 18.8 jit_solution(7731578076756580963)
XLA Ops:
  0.0 18.0 %shard_map.37 = bf16[1,128,2048]{2,1,0:T(8,128)(2,1)S(1)} custom-call(bf16[1,128,2048]{2,1,0:T(8,128)(2,1)} %q_hbm.1, bf16[1,128,512]{2,1,0:T(8,128)(2,1)} %k_hbm.1, bf16[1,128,512]{2,1,0:T(8,128)(2,1)} %v_hbm.1), custom_call_target="tpu_custom_call" | custom-call | tf_op jit(solution)/shard_map/pallas_call | solution.py:394
  18.0 0.8 %copy.5 = bf16[1,128,2048]{2,1,0:T(8,128)(2,1)} copy(bf16[1,128,2048]{2,1,0:T(8,128)(2,1)S(1)} %shard_map.37) | data formatting | bytes 1048576

commit v6 on v5

--- a/solution.py
+++ b/solution.py
@@ -65,7 +65,7 @@
     waiting = {g: rank for g in range(moved)} if rank == helper else {}
     seen = {g: [] for g in waiting}
     ready = set()
-    returned = 0
+    returned, later = 0, []
 
     def start_answer(g):
         ready.add(g)
@@ -92,7 +92,14 @@
                 how = {}
             seen[g].append(slot)
         ends = left[g] == 0 and not (rank == last and g < moved)
-        steps.append(pack(NEXT, slot, g, flag=FINISH if ends else KEEP, **how))
+        if g in waiting and waiting[g] and i + 1 < len(arrivals) and arrivals[i + 1][1] == g:
+            if how:
+                steps.append(pack(REST, slot, g, **how))
+            later.append(pack(NEXT, slot, g))
+        else:
+            steps += later
+            steps.append(pack(NEXT, slot, g, flag=FINISH if ends else KEEP, **how))
+            later = []
         for h in waiting:
             due = i + 1 < len(arrivals) and arrivals[i + 1][1] == h and waiting[h] == 1
             if h not in ready and (due or i >= taken_up(phase, h)):
@@ -103,7 +110,7 @@
                 returned += 1
     if rank == last:
         steps += [pack(MERGE, 0, g) for g in range(returned, moved)]
-    assert not queue
+    assert not queue and not later
     return before, steps, len(arrivals)
 
 

time: 19 us -> 18.8 us (0.989)
  no operation moved by 1% of the time
where the time goes in v6:
time: 18.8 us; the launch traced here: 18.7 us
  Pallas kernels  17.9 us (95%)
  local copies, waits for them, and re-layouts  0.8 us (4%)
    pallas_call x1, Pallas kernels, scheduled(): pl.pallas_call(functools.partial(scheduled_kernel, n, groups, per_group,...  17.9 us
    unnamed x1, local copies, waits for them, and re-layouts  0.8 us

profile of v6, /device:TPU:24, one launch (start us, length us, event | category | flops | bytes accessed | tf_op | source)
XLA Modules:
  0.0 18.7 jit_solution(14529896975141179999)
XLA Ops:
  0.0 17.9 %shard_map.37 = bf16[1,128,2048]{2,1,0:T(8,128)(2,1)S(1)} custom-call(bf16[1,128,2048]{2,1,0:T(8,128)(2,1)} %q_hbm.1, bf16[1,128,512]{2,1,0:T(8,128)(2,1)} %k_hbm.1, bf16[1,128,512]{2,1,0:T(8,128)(2,1)} %v_hbm.1), custom_call_target="tpu_custom_call" | custom-call | tf_op jit(solution)/shard_map/pallas_call | solution.py:401
  17.9 0.8 %copy.5 = bf16[1,128,2048]{2,1,0:T(8,128)(2,1)} copy(bf16[1,128,2048]{2,1,0:T(8,128)(2,1)S(1)} %shard_map.37) | data formatting | bytes 1048576

commit v7 on v6

--- a/solution.py
+++ b/solution.py
@@ -35,7 +35,7 @@
     own = [(top, g) for g in stay]
     older = [(b, g) for b in range(top - 1, -1, -1) for g in stay]
     away = [(b, g) for g in range(moved) for b in range(top, -1, -1)]
-    return own + older + away if phase == 0 else own + away + older
+    return own + older + away if phase == 0 else own + away[: top + 1] + older + away[top + 1 :][::-1]
 
 
 def taken_up(phase, g):

time: 18.8 us -> 18.8 us (level)
  no operation moved by 1% of the time
where the time goes in v7:
time: 18.8 us; the launch traced here: 18.7 us
  Pallas kernels  17.9 us (95%)
  local copies, waits for them, and re-layouts  0.8 us (4%)
    pallas_call x1, Pallas kernels, scheduled(): pl.pallas_call(functools.partial(scheduled_kernel, n, groups, per_group,...  17.9 us
    unnamed x1, local copies, waits for them, and re-layouts  0.8 us

profile of v7, /device:TPU:24, one launch (start us, length us, event | category | flops | bytes accessed | tf_op | source)
XLA Modules:
  0.0 18.7 jit_solution(14394352321951785010)
XLA Ops:
  0.0 17.9 %shard_map.37 = bf16[1,128,2048]{2,1,0:T(8,128)(2,1)S(1)} custom-call(bf16[1,128,2048]{2,1,0:T(8,128)(2,1)} %q_hbm.1, bf16[1,128,512]{2,1,0:T(8,128)(2,1)} %k_hbm.1, bf16[1,128,512]{2,1,0:T(8,128)(2,1)} %v_hbm.1), custom_call_target="tpu_custom_call" | custom-call | tf_op jit(solution)/shard_map/pallas_call | solution.py:401
  17.9 0.8 %copy.5 = bf16[1,128,2048]{2,1,0:T(8,128)(2,1)} copy(bf16[1,128,2048]{2,1,0:T(8,128)(2,1)S(1)} %shard_map.37) | data formatting | bytes 1048576
